TPU v7x, 32 devices: a whole 2x2x4 slice. The times are simulated.
32 devices in a mesh: grp: 4 (over z), seq: 8 (over y, x, core).
Axes of the slice: x: 2, y: 2, z: 4, core: 2. Of those that a mesh axis runs over, the one named last changes fastest.
Arguments:
- hidden_in: bfloat16 [24, 4096], P(None, ('grp', 'seq')), may hold values from -6 to 6
- norm_gain: float32 [4096], replicated, may hold values from 0.5 to 1.5
- w_ssm_in: bfloat16 [4096, 8192], P(None, ('grp', 'seq')), may hold values from -0.09375 to 0.09375
- w_ssm_gate: bfloat16 [4096, 8192], P(None, ('grp', 'seq')), may hold values from -0.09375 to 0.09375
- conv_weight: float32 [4, 8192], P(None, ('grp', 'seq')), may hold values from -3 to 3
- conv_bias: float32 [8192], P(('grp', 'seq')), may hold values from -0.5 to 0.5
- conv_state: bfloat16 [24, 3, 8192], P(None, None, ('grp', 'seq')), may hold values from -6 to 6
- w_state_proj: bfloat16 [8192, 288], P(('grp', 'seq')), may hold values from -0.0625 to 0.0625
- w_step: bfloat16 [256, 8192], P(None, ('grp', 'seq')), may hold values from -0.375 to 0.375
- step_bias: float32 [8192], P(('grp', 'seq')), may hold values from -4 to -1
- log_decay: float32 [16, 8192], P(None, ('grp', 'seq')), may hold values from 0 to 2.7
- skip_gain: float32 [8192], P(('grp', 'seq')), may hold values from 0.5 to 1.5
- ssm_state: float32 [24, 16, 8192], P(None, None, ('grp', 'seq')), may hold values from -6 to 6
- w_ssm_out: bfloat16 [8192, 4096], P(('grp', 'seq')), may hold values from -0.125 to 0.125
- w_query: bfloat16 [4096, 2048], P(None, 'grp'), may hold values from -6 to 6
- key_projection: bfloat16 [4096, 1024], P(None, 'grp'), may hold values from -0.09375 to 0.09375
- value_projection: bfloat16 [4096, 1024], P(None, 'grp'), may hold values from -0.09375 to 0.09375
- w_attn_out: bfloat16 [2048, 4096], P('grp', 'seq'), may hold values from -0.125 to 0.125
- w_mlp_gate: bfloat16 [4096, 14336], P(None, ('grp', 'seq')), may hold values from -0.09375 to 0.09375
- w_mlp_up: bfloat16 [4096, 14336], P(None, ('grp', 'seq')), may hold values from -0.09375 to 0.09375
- w_mlp_down: bfloat16 [14336, 4096], P(('grp', 'seq')), may hold values from -0.09375 to 0.09375
- cached_inputs: bfloat16 [24, 512, 4096], P('seq'), may hold values from -6 to 6
- window_lengths: int32 [24], replicated, may hold values from 1 to 512, as said below
Outputs:
- hidden_out: bfloat16 [24, 4096], P(None, ('grp', 'seq'))
- state_out: float32 [24, 16, 8192], P(None, None, ('grp', 'seq'))
Inputs may be any that keep to these rules, and one draw needn't show every extreme that they name: `window_lengths`: every sequence has at least one valid cached position, and some sequence fills the whole window of 512.
All inputs are finite; a program needn't handle non-finite values.
Results may differ from a plain program's by a relative error of at most 0.012.
The roundings to bfloat16 on the way count: a program that leaves them out, or rounds other values in their place, can miss the bound.
Values may be sent and summed in bfloat16 or wider, within the bound.
No kernel may reach another device: no remote copies, remote signals or barrier semaphores. Data moves between devices by JAX's collectives and lax.ppermute only.
A program may use at most 128 MiB of HBM per device.

v0:
```python
import jax
import jax.numpy as jnp
from jax import lax
from jax.sharding import PartitionSpec as P

HEAD_SIZE = 128
epsilon = 1e-05
rope_base = 10000.0


def apply_rotary(head_values, positions):
    half_dim = head_values.shape[-1] // 2
    frequency = rope_base ** (
        -(jnp.arange(half_dim, dtype=jnp.float32) * 2.0) / head_values.shape[-1]
    )
    angles = positions[..., None, None] * frequency
    cosine = jnp.cos(angles)
    sine_part = jnp.sin(angles)
    front_half = head_values[..., :half_dim]
    back_half = head_values[..., half_dim:]
    return jnp.concatenate(
        [front_half * cosine - back_half * sine_part, back_half * cosine + front_half * sine_part],
        axis=-1,
    )


def per_device(
    hidden_in,
    norm_gain,
    w_ssm_in,
    w_ssm_gate,
    conv_weight,
    conv_bias,
    conv_state,
    w_state_proj,
    w_step,
    step_bias,
    log_decay,
    skip_gain,
    ssm_state,
    w_ssm_out,
    w_query,
    key_projection,
    value_projection,
    w_attn_out,
    w_mlp_gate,
    w_mlp_up,
    w_mlp_down,
    cached_inputs,
    window_lengths,
):
    batch_rows = hidden_in.shape[0]
    model_width = norm_gain.shape[0]
    hidden_f = hidden_in.astype(jnp.float32)
    raw_full = lax.all_gather(hidden_in, ("grp", "seq"), axis=1, tiled=True).astype(jnp.float32)
    row_scale = lax.rsqrt(jnp.mean(raw_full * raw_full, axis=1, keepdims=True) + epsilon)
    normed_input = (raw_full * row_scale * norm_gain).astype(jnp.bfloat16)
    ssm_input = jnp.dot(normed_input, w_ssm_in, preferred_element_type=jnp.float32).astype(
        jnp.bfloat16
    )
    gate_input = jnp.dot(normed_input, w_ssm_gate, preferred_element_type=jnp.float32)
    past_inputs = conv_state.astype(jnp.float32)
    conv_sum = (
        conv_bias
        + jnp.sum(past_inputs * conv_weight[:-1][None], axis=1)
        + conv_weight[-1] * lax.optimization_barrier(ssm_input).astype(jnp.float32)
    )
    conv_out = jax.nn.silu(conv_sum)
    rank_size = w_step.shape[0]
    state_size = log_decay.shape[0]
    low_rank = lax.psum(
        jnp.dot(conv_out.astype(jnp.bfloat16), w_state_proj, preferred_element_type=jnp.float32),
        ("grp", "seq"),
    )
    step_low = low_rank[:, :rank_size].astype(jnp.bfloat16)
    input_map = low_rank[:, rank_size : rank_size + state_size]
    output_map = low_rank[:, rank_size + state_size :]
    step_size = jax.nn.softplus(
        jnp.dot(step_low, w_step, preferred_element_type=jnp.float32) + step_bias
    )
    decay_rate = jnp.exp(log_decay)
    state_out = (
        jnp.exp(-step_size[:, None, :] * decay_rate[None]) * ssm_state
        + step_size[:, None, :] * input_map[:, :, None] * conv_out[:, None, :]
    )
    ssm_mixed = jnp.sum(state_out * output_map[:, :, None], axis=1) + skip_gain * conv_out
    ssm_gated = (ssm_mixed * jax.nn.silu(gate_input)).astype(jnp.bfloat16)
    ssm_term = jnp.dot(ssm_gated, w_ssm_out, preferred_element_type=jnp.float32)
    ssm_summed = lax.psum_scatter(ssm_term, ("grp", "seq"), scatter_dimension=1, tiled=True)
    gate_act = jnp.dot(normed_input, w_mlp_gate, preferred_element_type=jnp.float32)
    up_act = jnp.dot(normed_input, w_mlp_up, preferred_element_type=jnp.float32)
    mlp_hidden = (jax.nn.silu(gate_act) * up_act).astype(jnp.bfloat16)
    mlp_term = jnp.dot(mlp_hidden, w_mlp_down, preferred_element_type=jnp.float32)
    own_seqs = cached_inputs.shape[0]
    window_size = cached_inputs.shape[1]
    seq_start = lax.axis_index("seq") * own_seqs
    normed_own = lax.dynamic_slice_in_dim(normed_input, seq_start, own_seqs, 0)
    lengths_own = lax.dynamic_slice_in_dim(window_lengths, seq_start, own_seqs, 0)
    heads_here = w_query.shape[1] // HEAD_SIZE
    kv_here = key_projection.shape[1] // HEAD_SIZE
    heads_per_group = heads_here // kv_here
    attention_scale = HEAD_SIZE ** (-0.5)
    fresh_position = lengths_own.astype(jnp.float32)
    query = apply_rotary(
        jnp.dot(normed_own, w_query, preferred_element_type=jnp.float32).reshape(
            own_seqs, heads_here, HEAD_SIZE
        ),
        fresh_position,
    ).astype(jnp.bfloat16)
    fresh_key = apply_rotary(
        jnp.dot(normed_own, key_projection, preferred_element_type=jnp.float32).reshape(
            own_seqs, kv_here, HEAD_SIZE
        ),
        fresh_position,
    ).astype(jnp.bfloat16)
    fresh_value = (
        jnp.dot(normed_own, value_projection, preferred_element_type=jnp.float32)
        .astype(jnp.bfloat16)
        .reshape(own_seqs, kv_here, HEAD_SIZE)
    )
    flat_inputs = cached_inputs.reshape(own_seqs * window_size, model_width)
    slot_ids = jnp.arange(window_size, dtype=jnp.int32)
    positions = jnp.broadcast_to(slot_ids[None, :], (own_seqs, window_size)).astype(jnp.float32)
    window_key_rows = jnp.dot(
        flat_inputs, key_projection, preferred_element_type=jnp.float32
    ).reshape(own_seqs, window_size, kv_here, HEAD_SIZE)
    window_key_rows = apply_rotary(window_key_rows, positions).astype(jnp.bfloat16)
    window_value_rows = (
        jnp.dot(flat_inputs, value_projection, preferred_element_type=jnp.float32)
        .astype(jnp.bfloat16)
        .reshape(own_seqs, window_size, kv_here, HEAD_SIZE)
    )
    grouped_query = query.astype(jnp.float32).reshape(own_seqs, kv_here, heads_per_group, HEAD_SIZE)
    scores = (
        jnp.einsum("bkgd,bpkd->bkgp", grouped_query, window_key_rows.astype(jnp.float32))
        * attention_scale
    )
    fresh_score = (
        jnp.einsum("ynow,ynw->yno", grouped_query, fresh_key.astype(jnp.float32)) * attention_scale
    )
    is_valid = (slot_ids[None, :] < lengths_own[:, None])[:, None, None, :]
    scores = jnp.where(is_valid, scores, -1e30)
    joint_max = jnp.maximum(jnp.max(scores, axis=-1), fresh_score)
    weights = jnp.where(is_valid, jnp.exp(scores - joint_max[..., None]), 0.0)
    weight_new = jnp.exp(fresh_score - joint_max)
    joint_total = jnp.sum(weights, axis=-1) + weight_new
    joint_sum = (
        jnp.einsum("bkgp,bpkd->bkgd", weights, window_value_rows.astype(jnp.float32))
        + weight_new[..., None] * fresh_value.astype(jnp.float32)[:, :, None, :]
    )
    attended_own = (
        (joint_sum / joint_total[..., None])
        .reshape(own_seqs, heads_here * HEAD_SIZE)
        .astype(jnp.bfloat16)
    )
    attended = lax.all_gather(attended_own, "seq", axis=0, tiled=True)
    attn_cols = jnp.dot(attended, w_attn_out, preferred_element_type=jnp.float32)
    col_start = lax.axis_index("seq") * w_attn_out.shape[1]
    attn_term = lax.dynamic_update_slice(
        jnp.zeros((batch_rows, model_width), jnp.float32), attn_cols, (jnp.int32(0), col_start)
    )
    other_terms = mlp_term + attn_term
    summed = ssm_summed + lax.psum_scatter(
        other_terms, ("grp", "seq"), scatter_dimension=1, tiled=True
    )
    hidden_out = (hidden_f + summed).astype(jnp.bfloat16)
    return (hidden_out, state_out)


def solution(mesh):
    placed = (
        P(None, ("grp", "seq")),
        P(),
        P(None, ("grp", "seq")),
        P(None, ("grp", "seq")),
        P(None, ("grp", "seq")),
        P(("grp", "seq")),
        P(None, None, ("grp", "seq")),
        P(("grp", "seq"), None),
        P(None, ("grp", "seq")),
        P(("grp", "seq")),
        P(None, ("grp", "seq")),
        P(("grp", "seq")),
        P(None, None, ("grp", "seq")),
        P(("grp", "seq"), None),
        P(None, "grp"),
        P(None, "grp"),
        P(None, "grp"),
        P("grp", "seq"),
        P(None, ("grp", "seq")),
        P(None, ("grp", "seq")),
        P(("grp", "seq"), None),
        P("seq", None, None),
        P(),
    )
    return jax.shard_map(
        per_device,
        mesh=mesh,
        in_specs=placed,
        out_specs=(P(None, ("grp", "seq")), P(None, None, ("grp", "seq"))),
        check_vma=False,
    )
```

profile of v0, /device:TPU:0, one launch (start us, length us, event | category | flops | bytes accessed | tf_op | source)
XLA Modules:
  0.0 289.1 jit_solution(317169863830582743)
XLA Ops:
  7.3 44.2 %all_gather.6 = bf16[24,4096]{1,0:T(8,128)(2,1)S(1)} all-gather(bf16[24,128]{1,0:T(8,128)(2,1)} %param.23), channel_id=1, replica_groups=mesh['grp'=4,'seq'=8] {'grp','seq'}, dimensions={1}, use_global_device_ids=true | all-gather | bytes 202752 | tf_op jit(solution)/shard_map/all_gather | solution.py:55
  51.4 0.2 fusion.13
  51.6 0.8 fusion.15
  52.5 2.8 fusion.25
  55.3 0.1 fusion.42
  55.5 0.1 multiply_cosine_fusion.1
  55.6 0.5 multiply_cosine_fusion
  56.1 2.0 fusion.23
  58.1 4.1 %copy.38 = bf16[256,4096]{1,0:T(8,128)(2,1)} copy(bf16[256,4096]{0,1:T(8,128)(2,1)} %bitcast.38) | data formatting | bytes 4194304 | tf_op jit(solution)/shard_map/dot_general | solution.py:124
  62.2 0.1 subtract_convert_fusion.1
  62.3 7.1 %fusion = f32[3,512,2,128]{1,3,2,0:T(8,128)S(1)} fusion(bf16[2,128,4096,1]{2,1,0,3:T(8,128)(2,1)} %bitcast.39, bf16[3,512,4096]{2,1,0:T(8,128)(2,1)} %param.44), kind=kOutput, calls=%fused_computation | convolution fusion | flops 3221225472 | bytes 16252928 | tf_op jit(solution)/shard_map/dot_general | solution.py:124
  69.5 0.1 maximum_bitcast_fusion
  69.6 0.3 subtract_convert_fusion
  69.9 0.2 fusion.32
  70.1 0.3 fusion.44
  70.5 0.2 fusion.31
  70.7 0.4 fusion.8
  71.1 7.4 %convolution_convert_fusion = bf16[1536,256]{1,0:T(8,128)(2,1)} fusion(bf16[1536,4096]{1,0:T(8,128)(2,1)} %bitcast.48, bf16[4096,256]{1,0:T(8,128)(2,1)S(1)} %copy-done), kind=kOutput, calls=%fused_computation.3 | convolution fusion | flops 3221618688 | bytes 15466496 | tf_op jit(solution)/shard_map/dot_general | solution.py:129
  78.4 2.0 reshape.155
  80.5 0.3 fusion.7
  80.8 7.0 %all-gather = bf16[8,3,512]{2,1,0:T(4,128)(2,1)S(1)} all-gather(bf16[1,3,512]{2,1,0:T(4,128)(2,1)S(1)} %reshape.157), channel_id=1, replica_groups=mesh['grp'=4,'seq'=8] {'seq'}, dimensions={0}, use_global_device_ids=true | all-gather | bytes 27648 | tf_op jit(solution)/shard_map/all_gather | solution.py:156
  87.8 3.1 %fusion.48 = f32[24,448]{1,0:T(8,128)S(1)} fusion(bf16[24,4096]{1,0:T(8,128)(2,1)S(1)} %fusion.15, bf16[4096,448]{0,1:T(8,128)(2,1)} %param.41), kind=kOutput, calls=%fused_computation.85 | convolution fusion | flops 88080384 | bytes 3909632 | tf_op jit(solution)/shard_map/dot_general | solution.py:90
  91.0 2.1 convolution_convert_fusion.1
  93.2 0.2 fusion.28
  93.4 38.3 %psum.7 = f32[24,288]{1,0:T(8,128)S(1)} all-reduce(f32[24,288]{1,0:T(8,128)S(1)} %fusion.28), channel_id=1, replica_groups=mesh['grp'=4,'seq'=8] {'grp','seq'}, use_global_device_ids=true, to_apply=%region_2.3 | all-reduce | flops 6912 | bytes 55296 | tf_op jit(solution)/shard_map/psum | solution.py:71
  131.8 0.2 fusion.45
  132.0 5.1 %fusion.4 = f32[24,4096]{1,0:T(8,128)S(1)} fusion(bf16[448,4096]{1,0:T(8,128)(2,1)} %param.43, bf16[24,4096]{1,0:T(8,128)(2,1)S(1)} %fusion.15, bf16[4096,448]{0,1:T(8,128)(2,1)} %param.42, f32[24,448]{1,0:T(8,128)S(1)} %fusion.48), kind=kOutput, calls=%fused_computation.8 | convolution fusion | flops 176225280 | bytes 7972864 | tf_op jit(solution)/shard_map/dot_general | solution.py:93
  137.1 0.2 fusion.2
  137.3 1.9 multiply_reduce_fusion
  139.3 4.3 %convolution_add_fusion = f32[24,4096]{1,0:T(8,128)} fusion(f32[24,4096]{1,0:T(8,128)S(1)} %fusion.2, bf16[256,4096]{1,0:T(8,128)(2,1)} %param.36, f32[24,256]{1,0:T(8,128)S(1)} %get-tuple-element.2, f32[24,256]{1,0:T(8,128)S(1)} %divide_multiply_fusion, f32[256]{0:T(256)S(1)} %copy-done.10, bf16[24,4096]{1,0:T(8,128)(2,1)S(1)} %fusion.15, ...), kind=kOutput, calls=%fused_computation.2 | convolution fusion | flops 100810752 | bytes 5227520 | tf_op jit(solution)/shard_map/dot_general | solution.py:88
  143.6 137.4 %reduce-scatter.2.cloned.1.call-done = f32[24,128]{1,0:T(8,128)} async-done(((f32[24,4096]{1,0:T(8,128)}), f32[24,128]{1,0:T(8,128)}) %reduce-scatter.2.cloned.1.call-update) | async-done | bytes 12304 | tf_op jit(solution)/shard_map/reduce_scatter | solution.py:89
  280.9 1.3 add_convert_fusion.1
  (43 shorter events, 0.6 us)
Async XLA Ops:
  7.2 63.5 %copy-start = (bf16[4096,256]{1,0:T(8,128)(2,1)S(1)}, bf16[4096,256]{1,0:T(8,128)(2,1)}, u32[]{:S(2)}) copy-start(bf16[4096,256]{1,0:T(8,128)(2,1)} %param.39) | copy-start | bytes 6291460
  7.2 273.8 %reduce-scatter.2.cloned.1.call-start = ((), (), s32[]{:S(2)}) async-start(), calls=%async_computation.1 | async-start | bytes 405504 | tf_op jit(solution)/shard_map/reduce_scatter | solution.py:89
  52.4 2.9 copy-start.11
  90.9 2.2 copy-start.7
  90.9 2.2 copy-start.4
  91.0 2.2 copy-start.8
  91.0 2.2 copy-start.2
  91.0 40.8 %copy-start.6 = (f32[16,256]{1,0:T(8,128)S(1)}, f32[16,256]{1,0:T(8,128)}, u32[]{:S(2)}) copy-start(f32[16,256]{1,0:T(8,128)} %param.33) | copy-start | bytes 49156
  91.0 40.8 %copy-start.3 = (bf16[256,256]{1,0:T(8,128)(2,1)S(1)}, bf16[256,256]{1,0:T(8,128)(2,1)}, u32[]{:S(2)}) copy-start(bf16[256,256]{1,0:T(8,128)(2,1)} %param.31) | copy-start | bytes 393220
  91.0 40.8 %copy-start.9 = (f32[256]{0:T(256)S(1)}, f32[256]{0:T(256)}, u32[]{:S(2)}) copy-start(f32[256]{0:T(256)} %param.32) | copy-start | bytes 3076
  132.0 5.1 %copy-start.1 = (bf16[512,512]{1,0:T(8,128)(2,1)S(1)}, bf16[512,512]{1,0:T(8,128)(2,1)}, u32[]{:S(2)}) copy-start(bf16[512,512]{1,0:T(8,128)(2,1)} %param.40) | copy-start | bytes 1572868
  132.0 7.2 %copy-start.10 = (f32[256]{0:T(256)S(1)}, f32[256]{0:T(256)}, u32[]{:S(2)}) copy-start(f32[256]{0:T(256)} %param.34) | copy-start | bytes 3076
  139.3 141.7 %copy-start.5 = (bf16[24,128]{1,0:T(8,128)(2,1)S(1)}, bf16[24,128]{1,0:T(8,128)(2,1)}, u32[]{:S(2)}) copy-start(bf16[24,128]{1,0:T(8,128)(2,1)} %param.23) | copy-start | bytes 18436
Sparse Core Ops, SparseCore 0:
  143.7 137.2 reduce-scatter.1
where the time goes:
time: 290 us; the launch traced here: 289 us
  waiting for transfers between devices  137 us (47%)
  blocking collectives  89.5 us (31%)
  matrix products  35.6 us (12%)
  between operations  14.3 us (5%)
  local copies, waits for them, and re-layouts  6.37 us (2%)
  other arithmetic  5.87 us (2%)
    reduce_scatter x1, waiting for transfers between devices, per_device(): lax.psum_scatter(ssm_term, ('grp', 'seq'), scatter_dimension=1, tiled=True)  137 us
    all_gather x1, blocking collectives, per_device(): lax.all_gather(hidden_in, ('grp', 'seq'), axis=1, tiled=True)  44.2 us
    psum x1, blocking collectives, per_device(): lax.psum(jnp.dot(conv_out.astype(jnp.bfloat16), w_state_proj, preferred_e...  38.3 us
    dot_general x1, matrix products, per_device(): jnp.dot(flat_inputs, value_projection, preferred_element_type=jnp.float32)  7.38 us
    dot_general x1, matrix products, per_device(): jnp.dot(flat_inputs, key_projection, preferred_element_type=jnp.float32)  7.13 us
    all_gather x1, blocking collectives, per_device(): attended = lax.all_gather(attended_own, 'seq', axis=0, tiled=True)  7.02 us
  transfers between devices with their start and end apart: 1, of which 1 were waited for; matrix products, arithmetic and copies ran while one was open for 0% of the time, Pallas kernels for 0%

commit v1 on v0

--- a/solution.py
+++ b/solution.py
@@ -68,10 +68,11 @@
     conv_out = jax.nn.silu(conv_sum)
     rank_size = w_step.shape[0]
     state_size = log_decay.shape[0]
-    low_rank = lax.psum(
-        jnp.dot(conv_out.astype(jnp.bfloat16), w_state_proj, preferred_element_type=jnp.float32),
-        ("grp", "seq"),
-    )
+    low_rank = jnp.dot(
+        conv_out.astype(jnp.bfloat16), w_state_proj, preferred_element_type=jnp.float32
+    )
+    for mesh_axis in ("seq", "grp"):
+        low_rank = lax.psum(low_rank, mesh_axis)
     step_low = low_rank[:, :rank_size].astype(jnp.bfloat16)
     input_map = low_rank[:, rank_size : rank_size + state_size]
     output_map = low_rank[:, rank_size + state_size :]

time: 290 us -> 290 us (level)
    psum x1 -> x2, blocking collectives: 38.3 us -> 41.1 us  [per_device(): low_rank = lax.psum(low_rank, mesh_axis)]
where the time goes in v1:
time: 290 us; the launch traced here: 289 us
  waiting for transfers between devices  135 us (47%)
  blocking collectives  92.3 us (32%)
  matrix products  35.6 us (12%)
  between operations  14.3 us (5%)
  local copies, waits for them, and re-layouts  6.4 us (2%)
  other arithmetic  5.87 us (2%)
    reduce_scatter x1, waiting for transfers between devices, per_device(): lax.psum_scatter(ssm_term, ('grp', 'seq'), scatter_dimension=1, tiled=True)  135 us
    all_gather x1, blocking collectives, per_device(): lax.all_gather(hidden_in, ('grp', 'seq'), axis=1, tiled=True)  44.2 us
    psum x2, blocking collectives, per_device(): low_rank = lax.psum(low_rank, mesh_axis)  41.1 us
    dot_general x1, matrix products, per_device(): jnp.dot(flat_inputs, value_projection, preferred_element_type=jnp.float32)  7.38 us
    dot_general x1, matrix products, per_device(): jnp.dot(flat_inputs, key_projection, preferred_element_type=jnp.float32)  7.14 us
    all_gather x1, blocking collectives, per_device(): attended = lax.all_gather(attended_own, 'seq', axis=0, tiled=True)  7.02 us
  transfers between devices with their start and end apart: 1, of which 1 were waited for; matrix products, arithmetic and copies ran while one was open for 0% of the time, Pallas kernels for 0%

profile of v1, /device:TPU:0, one launch (start us, length us, event | category | flops | bytes accessed | tf_op | source)
XLA Modules:
  0.0 289.2 jit_solution(6163291654230625179)
XLA Ops:
  7.3 44.2 %all_gather.6 = bf16[24,4096]{1,0:T(8,128)(2,1)S(1)} all-gather(bf16[24,128]{1,0:T(8,128)(2,1)} %param.23), channel_id=1, replica_groups=mesh['grp'=4,'seq'=8] {'grp','seq'}, dimensions={1}, use_global_device_ids=true | all-gather | bytes 202752 | tf_op jit(solution)/shard_map/all_gather | solution.py:55
  51.4 0.2 fusion.13
  51.6 0.8 fusion.15
  52.5 2.8 fusion.25
  55.3 0.1 fusion.42
  55.5 0.1 multiply_cosine_fusion.1
  55.6 0.5 multiply_cosine_fusion
  56.1 2.0 fusion.23
  58.1 4.1 %copy.38 = bf16[256,4096]{1,0:T(8,128)(2,1)} copy(bf16[256,4096]{0,1:T(8,128)(2,1)} %bitcast.38) | data formatting | bytes 4194304 | tf_op jit(solution)/shard_map/dot_general | solution.py:125
  62.4 7.1 %fusion = f32[3,512,2,128]{1,3,2,0:T(8,128)S(1)} fusion(bf16[2,128,4096,1]{2,1,0,3:T(8,128)(2,1)} %bitcast.39, bf16[3,512,4096]{2,1,0:T(8,128)(2,1)} %param.44), kind=kOutput, calls=%fused_computation | convolution fusion | flops 3221225472 | bytes 16252928 | tf_op jit(solution)/shard_map/dot_general | solution.py:125
  69.5 0.1 maximum_bitcast_fusion
  69.6 0.3 subtract_convert_fusion
  69.9 0.2 fusion.32
  70.1 0.3 fusion.44
  70.5 0.2 fusion.31
  70.7 0.4 fusion.8
  71.1 7.4 %convolution_convert_fusion = bf16[1536,256]{1,0:T(8,128)(2,1)} fusion(bf16[1536,4096]{1,0:T(8,128)(2,1)} %bitcast.48, bf16[4096,256]{1,0:T(8,128)(2,1)S(1)} %copy-done), kind=kOutput, calls=%fused_computation.3 | convolution fusion | flops 3221618688 | bytes 15466496 | tf_op jit(solution)/shard_map/dot_general | solution.py:130
  78.5 2.0 reshape.155
  80.5 0.3 fusion.7
  80.8 7.0 %all-gather = bf16[8,3,512]{2,1,0:T(4,128)(2,1)S(1)} all-gather(bf16[1,3,512]{2,1,0:T(4,128)(2,1)S(1)} %reshape.157), channel_id=1, replica_groups=mesh['grp'=4,'seq'=8] {'seq'}, dimensions={0}, use_global_device_ids=true | all-gather | bytes 27648 | tf_op jit(solution)/shard_map/all_gather | solution.py:157
  87.9 3.1 %fusion.48 = f32[24,448]{1,0:T(8,128)S(1)} fusion(bf16[24,4096]{1,0:T(8,128)(2,1)S(1)} %fusion.15, bf16[4096,448]{0,1:T(8,128)(2,1)} %param.41), kind=kOutput, calls=%fused_computation.85 | convolution fusion | flops 88080384 | bytes 3909632 | tf_op jit(solution)/shard_map/dot_general | solution.py:91
  91.1 2.1 convolution_convert_fusion.1
  93.2 0.2 fusion.28
  93.4 24.8 %psum.14 = f32[24,288]{1,0:T(8,128)S(1)} all-reduce(f32[24,288]{1,0:T(8,128)S(1)} %fusion.28), channel_id=1, replica_groups=mesh['grp'=4,'seq'=8] {'seq'}, use_global_device_ids=true, to_apply=%region_2.3 | all-reduce | flops 6912 | bytes 55296 | tf_op jit(solution)/shard_map/psum | solution.py:75
  118.2 16.2 %psum.15 = f32[24,288]{1,0:T(8,128)S(1)} all-reduce(f32[24,288]{1,0:T(8,128)S(1)} %psum.14), channel_id=1, replica_groups=mesh['grp'=4,'seq'=8] {'grp'}, use_global_device_ids=true, to_apply=%region_3.4 | all-reduce | flops 6912 | bytes 55296 | tf_op jit(solution)/shard_map/psum | solution.py:75
  134.6 0.2 fusion.45
  134.8 5.1 %fusion.4 = f32[24,4096]{1,0:T(8,128)S(1)} fusion(bf16[448,4096]{1,0:T(8,128)(2,1)} %param.43, bf16[24,4096]{1,0:T(8,128)(2,1)S(1)} %fusion.15, bf16[4096,448]{0,1:T(8,128)(2,1)} %param.42, f32[24,448]{1,0:T(8,128)S(1)} %fusion.48), kind=kOutput, calls=%fused_computation.8 | convolution fusion | flops 176225280 | bytes 7972864 | tf_op jit(solution)/shard_map/dot_general | solution.py:94
  139.9 0.2 fusion.2
  140.1 1.9 multiply_reduce_fusion
  142.0 4.3 %convolution_add_fusion = f32[24,4096]{1,0:T(8,128)} fusion(f32[24,4096]{1,0:T(8,128)S(1)} %fusion.2, bf16[256,4096]{1,0:T(8,128)(2,1)} %param.36, f32[24,256]{1,0:T(8,128)S(1)} %get-tuple-element.2, f32[24,256]{1,0:T(8,128)S(1)} %divide_multiply_fusion, f32[256]{0:T(256)S(1)} %copy-done.10, bf16[24,4096]{1,0:T(8,128)(2,1)S(1)} %fusion.15, ...), kind=kOutput, calls=%fused_computation.2 | convolution fusion | flops 100810752 | bytes 5227520 | tf_op jit(solution)/shard_map/dot_general | solution.py:89
  146.4 134.7 %reduce-scatter.2.cloned.1.call-done = f32[24,128]{1,0:T(8,128)} async-done(((f32[24,4096]{1,0:T(8,128)}), f32[24,128]{1,0:T(8,128)}) %reduce-scatter.2.cloned.1.call-update) | async-done | bytes 12304 | tf_op jit(solution)/shard_map/reduce_scatter | solution.py:90
  281.1 1.3 add_convert_fusion.1
  (44 shorter events, 0.6 us)
Async XLA Ops:
  7.2 63.5 %copy-start = (bf16[4096,256]{1,0:T(8,128)(2,1)S(1)}, bf16[4096,256]{1,0:T(8,128)(2,1)}, u32[]{:S(2)}) copy-start(bf16[4096,256]{1,0:T(8,128)(2,1)} %param.39) | copy-start | bytes 6291460
  7.2 273.9 %reduce-scatter.2.cloned.1.call-start = ((), (), s32[]{:S(2)}) async-start(), calls=%async_computation.1 | async-start | bytes 405504 | tf_op jit(solution)/shard_map/reduce_scatter | solution.py:90
  52.4 2.9 copy-start.11
  91.0 2.2 copy-start.7
  91.0 2.2 copy-start.4
  91.0 2.2 copy-start.8
  91.0 2.2 copy-start.2
  91.0 43.5 %copy-start.6 = (f32[16,256]{1,0:T(8,128)S(1)}, f32[16,256]{1,0:T(8,128)}, u32[]{:S(2)}) copy-start(f32[16,256]{1,0:T(8,128)} %param.33) | copy-start | bytes 49156
  91.0 43.5 %copy-start.3 = (bf16[256,256]{1,0:T(8,128)(2,1)S(1)}, bf16[256,256]{1,0:T(8,128)(2,1)}, u32[]{:S(2)}) copy-start(bf16[256,256]{1,0:T(8,128)(2,1)} %param.31) | copy-start | bytes 393220
  91.0 43.5 %copy-start.9 = (f32[256]{0:T(256)S(1)}, f32[256]{0:T(256)}, u32[]{:S(2)}) copy-start(f32[256]{0:T(256)} %param.32) | copy-start | bytes 3076
  134.8 5.1 %copy-start.1 = (bf16[512,512]{1,0:T(8,128)(2,1)S(1)}, bf16[512,512]{1,0:T(8,128)(2,1)}, u32[]{:S(2)}) copy-start(bf16[512,512]{1,0:T(8,128)(2,1)} %param.40) | copy-start | bytes 1572868
  134.8 7.2 %copy-start.10 = (f32[256]{0:T(256)S(1)}, f32[256]{0:T(256)}, u32[]{:S(2)}) copy-start(f32[256]{0:T(256)} %param.34) | copy-start | bytes 3076
  142.0 139.1 %copy-start.5 = (bf16[24,128]{1,0:T(8,128)(2,1)S(1)}, bf16[24,128]{1,0:T(8,128)(2,1)}, u32[]{:S(2)}) copy-start(bf16[24,128]{1,0:T(8,128)(2,1)} %param.23) | copy-start | bytes 18436
Sparse Core Ops, SparseCore 0:
  146.5 134.5 reduce-scatter.1
